TPU v7x, 256 devices: a whole 4x4x8 slice. The times are simulated.
256 devices in a mesh: prow: 16 (over z, core), pcol: 16 (over x, y).
Axes of the slice: x: 4, y: 4, z: 8, core: 2. Of those that a mesh axis runs over, the one named last changes fastest.
Arguments:
- inv_lead: float32 [4, 16, 256, 4, 16, 256], P(None, 'prow', None, None, 'pcol'), may hold values from -1 to 2, as said below
- h_lead: float32 [4, 16, 256, 6, 16, 256], P(None, 'pcol', None, None, 'prow'), may hold values from -6 to 6
- h_slab: float32 [512, 6, 16, 256], P('pcol', None, 'prow'), may hold values from -6 to 6
- l_panel: float32 [512, 4, 16, 256], P('pcol', None, 'prow'), may hold values from -0.046875 to 0.046875
- l_diag: float32 [512, 512], replicated, may hold values from -1 to 2, as said below
Outputs:
- x_slab: float32 [512, 6, 16, 256], P('pcol', None, 'prow')
- y_lead: float32 [512, 4, 16, 256], P('pcol', None, 'prow')
- y_diag: float32 [512, 512], P('pcol', 'prow')
Inputs may be any that keep to these rules, and one draw needn't show every extreme that they name: inv_lead is lower triangular in natural order, with diagonal entries between 1 and 2. l_diag is lower triangular, with diagonal entries between 1 and 2.
All inputs are finite; a program needn't handle non-finite values.
Results may differ from a plain program's by a relative error of at most 0.00018.
Values sent between devices are 32-bit elements; how exact they have to be, the bound alone decides.
No kernel may reach another device: no remote copies, remote signals or barrier semaphores. Data moves between devices by JAX's collectives and lax.ppermute only.
A program may use at most 128 MiB of HBM per device.

v0:
```python
import jax
import jax.numpy as jnp
from jax import lax
from jax.sharding import PartitionSpec as P


def copy_for_each(value, axis):
    copies = jnp.broadcast_to(value, (lax.axis_size(axis), *value.shape))
    return lax.all_to_all(copies, axis, split_axis=0, concat_axis=0, tiled=True)


def joined_along(parts, dim):
    lengths = list(parts.shape[1:])
    lengths[dim] *= parts.shape[0]
    return jnp.moveaxis(parts, 0, dim).reshape(lengths)


def gathered_copies(value, axis, dim):
    parts = copy_for_each(value, axis)
    return joined_along(parts, dim)


def in_blocks(value, dim, size):
    lengths = value.shape
    parts = value.reshape(*lengths[:dim], size, lengths[dim] // size, *lengths[dim + 1 :])
    return jnp.moveaxis(parts, dim, 0)


def sum_at_owner(value, axis, dim):
    parts = in_blocks(value, dim, lax.axis_size(axis))
    arrived = lax.all_to_all(parts, axis, split_axis=0, concat_axis=0, tiled=True)
    return arrived.sum(axis=0)


def in_one_piece(arrays, axis, dim, along):
    widths = [a.shape[along] for a in arrays]
    both = jnp.concatenate(arrays, axis=along)
    result = lax.psum_scatter(both, axis, scatter_dimension=dim, tiled=True)
    return tuple(jnp.split(result, [sum(widths[:k]) for k in range(1, len(widths))], axis=along))


def matmul_hi(left, right):
    return jnp.dot(left, right, precision=lax.Precision.HIGHEST, preferred_element_type=jnp.float32)


def matmul_trans(left, right):
    return lax.dot_general(
        left,
        right,
        (((1,), (1,)), ((), ())),
        precision=lax.Precision.HIGHEST,
        preferred_element_type=jnp.float32,
    )


def invert_diag(l_diag, block_size):
    diag_top = l_diag[:block_size, :block_size]
    diag_bottom = l_diag[block_size:, block_size:]
    off_block = l_diag[block_size:, :block_size]
    identity = jnp.eye(block_size, dtype=jnp.float32)
    top_inv = lax.linalg.triangular_solve(diag_top, identity, left_side=True, lower=True)
    bottom_inv = lax.linalg.triangular_solve(diag_bottom, identity, left_side=True, lower=True)
    corner = -matmul_hi(bottom_inv, matmul_hi(off_block, top_inv))
    upper_rows = jnp.concatenate([top_inv, jnp.zeros_like(top_inv)], axis=1)
    lower_rows = jnp.concatenate([corner, bottom_inv], axis=1)
    return jnp.concatenate([upper_rows, lower_rows], axis=0)


def per_device(inv_lead, h_lead, h_slab, l_panel, l_diag):
    slab_rows = l_diag.shape[0]
    block_size = l_panel.shape[3]
    prev_blocks = l_panel.shape[1]
    x_rows = l_panel.shape[0]
    h_blocks = h_slab.shape[1]
    diag_inv = invert_diag(l_diag, slab_rows // 2)
    inv_local = inv_lead.reshape(prev_blocks * block_size, -1)
    col_width = inv_local.shape[1]
    col_blocks = col_width // block_size
    h_local = h_lead.reshape(col_width, -1)
    h_side = h_slab.reshape(x_rows, -1)
    y_rows = slab_rows // lax.axis_size("prow")
    row_start = lax.axis_index("prow") * y_rows
    col_start = lax.axis_index("pcol") * x_rows
    piece = gathered_copies(l_panel, "pcol", 0)
    factor = matmul_hi(diag_inv, piece.reshape(piece.shape[0], -1))
    side_term = matmul_hi(lax.dynamic_slice_in_dim(diag_inv, col_start, x_rows, 1), h_side)
    own_panel = sum_at_owner(-matmul_hi(factor, inv_local), "prow", 0)
    product = matmul_hi(lax.all_gather(own_panel, "prow", axis=0, tiled=True), h_local)
    x_local = sum_at_owner(product + side_term, "pcol", 0)
    x_slab = x_local.reshape(x_rows, h_blocks, 1, block_size)
    kept_cols = x_slab[:, : prev_blocks + 1]
    widened = lax.all_gather(kept_cols, "prow", axis=2, tiled=True).reshape(x_rows, -1)
    prev_rows = prev_blocks * block_size * lax.axis_size("prow")
    head_cols = widened[:, :prev_rows]
    tail_cols = widened[:, prev_rows : prev_rows + slab_rows]
    shifted_x = lax.all_to_all(
        head_cols.reshape(x_rows, col_blocks, lax.axis_size("pcol"), block_size),
        "pcol",
        split_axis=2,
        concat_axis=0,
        tiled=True,
    )
    shifted_x = shifted_x.reshape(slab_rows, col_width)
    lead_part = matmul_trans(shifted_x, inv_local)
    diag_part = matmul_trans(shifted_x, own_panel)
    y_first, y_block = in_one_piece((lead_part, diag_part), "pcol", 0, 1)
    diag_rows = lax.dynamic_slice_in_dim(diag_inv, row_start, y_rows, 0)
    y_diag = y_block + matmul_trans(tail_cols, diag_rows)
    return (x_slab, y_first.reshape(x_rows, prev_blocks, 1, block_size), y_diag)


def solution(mesh):
    return jax.shard_map(
        per_device,
        mesh=mesh,
        in_specs=(
            P(None, "prow", None, None, "pcol", None),
            P(None, "pcol", None, None, "prow", None),
            P("pcol", None, "prow", None),
            P("pcol", None, "prow", None),
            P(),
        ),
        out_specs=(P("pcol", None, "prow", None), P("pcol", None, "prow", None), P("pcol", "prow")),
        check_vma=False,
    )
```

profile of v0, /device:TPU:2, one launch (start us, length us, event | category | flops | bytes accessed | tf_op | source)
XLA Modules:
  0.0 457.1 jit_solution(1383191247335577584)
XLA Ops:
  8.1 2.9 broadcast_in_dim.4
  11.1 7.5 %all-to-all-start = ((f32[16,32,4,1,256]{4,3,2,1,0:T(1,128)}), f32[16,32,4,1,256]{4,3,2,1,0:T(1,128)S(1)}, u32[]{:S(2)}, u32[]{:S(2)}) async-start(f32[16,32,4,1,256]{4,3,2,1,0:T(1,128)} %broadcast_in_dim.4), calls=%async_computation | async-start | bytes 4194304 | tf_op jit(solution)/shard_map/all_to_all | solution.py:9
  19.8 3.8 while.4
  23.6 19.7 %custom-call.4 = f32[2,128,128]{1,2,0:T(8,128)S(1)} custom-call(f32[2,128,128]{2,1,0:T(8,128)S(1)} %get-tuple-element.18), custom_call_target="InvertDiagBlocksLowerTriangular" | custom-call | tf_op jit(solution)/shard_map/triangular_solve/custom-call.1 | solution.py:61
  43.3 4.0 while.5
  47.3 19.7 %custom-call.5 = f32[2,128,128]{1,2,0:T(8,128)S(1)} custom-call(f32[2,128,128]{2,1,0:T(8,128)S(1)} %get-tuple-element.19), custom_call_target="InvertDiagBlocksLowerTriangular" | custom-call | tf_op jit(solution)/shard_map/triangular_solve/custom-call.1 | solution.py:62
  67.0 14.2 %reduce.1 = f32[4,256,4,256]{3,2,1,0:T(4,128)} reduce(f32[4,1,256,4,1,256]{5,4,3,2,1,0:T(1,128)} %param.7, f32[]{:T(128)} %constant.47), dimensions={1,4}, to_apply=%param.7.reduce_sub_computation | reduce | bytes 8388612 | tf_op args[0]
  81.2 5.2 %copy.34 = f32[128,8,4,256]{3,1,2,0:T(8,128)} copy(f32[128,8,4,256]{3,2,1,0:T(4,128)} %bitcast.82) | data formatting | bytes 8388608
  90.2 7.4 %reduce = f32[16,32,4,256]{3,2,1,0:T(4,128)} reduce(f32[16,32,4,1,256]{4,3,2,1,0:T(1,128)S(1)} %all-to-all-done, f32[]{:T(128)} %constant.47), dimensions={3}, to_apply=%all_to_all.20.reduce_sub_computation | reduce | bytes 4194308 | tf_op jit(solution)/shard_map/all_to_all | solution.py:9
  97.6 2.1 copy.33
  99.7 4.0 fusion.22
  103.7 6.9 %convolution_negate_fusion = f32[512,1024]{1,0:T(8,128)S(1)} fusion(f32[512,1024]{1,0:T(8,128)S(1)} %fusion.22, f32[1024,1024]{1,0:T(8,128)S(1)} %bitcast.77), kind=kOutput, calls=%fused_computation.6 | convolution fusion | flops 6442975232 | bytes 8388608 | tf_op jit(solution)/shard_map/dot_general | solution.py:43
  110.6 58.0 %all_to_all.31 = f32[16,32,1024]{2,1,0:T(8,128)S(1)} all-to-all(f32[16,32,1024]{2,1,0:T(8,128)S(1)} %bitcast.92), channel_id=1, replica_groups=mesh['prow'=16,'pcol'=16] {'prow'}, dimensions={0} | all-to-all | bytes 4194304 | tf_op jit(solution)/shard_map/all_to_all | solution.py:31
  169.5 37.4 %reduce.2 = f32[4,256,6,256]{3,2,1,0:T(8,128)} reduce(f32[4,1,256,6,1,256]{5,4,3,2,1,0:T(1,128)} %param.8, f32[]{:T(128)} %constant.47), dimensions={1,4}, to_apply=%param.8.reduce_sub_computation | reduce | bytes 12582916 | tf_op args[1]
  206.8 9.2 %copy.35 = f32[128,8,6,256]{3,1,2,0:T(8,128)} copy(f32[128,8,6,256]{3,2,1,0:T(8,128)} %bitcast.79) | data formatting | bytes 12582912
  216.8 13.7 %fusion.25 = f32[512,1536]{1,0:T(8,128)S(1)} fusion(f32[512,1024]{1,0:T(8,128)} %all-gather.3.cloned.1.call-done, f32[1024,1536]{1,0:T(8,128)} %bitcast.93), kind=kOutput, calls=%fused_computation.47 | convolution fusion | flops 9663676416 | bytes 11534336 | tf_op jit(solution)/shard_map/dot_general | solution.py:43
  230.4 2.8 convolution_add_fusion
  233.2 45.1 %all_to_all.32 = f32[16,32,1536]{2,1,0:T(8,128)S(1)} all-to-all(f32[16,32,1536]{2,1,0:T(8,128)S(1)} %bitcast.83), channel_id=1, replica_groups=mesh['prow'=16,'pcol'=16] {'pcol'}, dimensions={0} | all-to-all | bytes 6291456 | tf_op jit(solution)/shard_map/all_to_all | solution.py:31
  279.4 36.6 %all-gather.5.cloned.1.call-done = f32[32,5,16,256]{3,0,1,2:T(8,128)} async-done(((f32[32,5,1,256]{3,0,1,2:T(8,128)}), f32[32,5,16,256]{3,0,1,2:T(8,128)}) %all-gather.5.cloned.1.call-update) | async-done | bytes 2621456 | tf_op jit(solution)/shard_map/all_gather | solution.py:92
  315.9 3.3 copy.25
  322.9 33.8 %all_to_all.30 = f32[32,4,16,256]{3,1,0,2:T(4,128)S(1)} all-to-all(f32[32,4,16,256]{3,1,0,2:T(4,128)S(1)} %copy.26), channel_id=1, replica_groups=mesh['prow'=16,'pcol'=16] {'pcol'}, dimensions={2} | all-to-all | bytes 4194304 | tf_op jit(solution)/shard_map/all_to_all | solution.py:96
  358.8 7.0 %fusion.26 = f32[512,1024]{1,0:T(8,128)S(1)} fusion(f32[512,1024]{1,0:T(8,128)S(1)} %bitcast.80, f32[1024,1024]{1,0:T(8,128)S(1)} %bitcast.78), kind=kOutput, calls=%fused_computation.48 | convolution fusion | flops 6442450944 | bytes 8388608 | tf_op jit(solution)/shard_map/dot_general | solution.py:47
  365.8 1.8 fusion.27
  370.1 76.6 %reduce-scatter.2.cloned.1.call-done = f32[32,1056]{1,0:T(8,128)} async-done(((f32[512,1056]{1,0:T(8,128)}), f32[32,1056]{1,0:T(8,128)}) %reduce-scatter.2.cloned.1.call-update) | async-done | bytes 135184 | tf_op jit(solution)/shard_map/reduce_scatter | solution.py:38
  (63 shorter events, 27.8 us)
Async XLA Ops:
  11.1 79.2 %all-to-all-start = ((f32[16,32,4,1,256]{4,3,2,1,0:T(1,128)}), f32[16,32,4,1,256]{4,3,2,1,0:T(1,128)S(1)}, u32[]{:S(2)}, u32[]{:S(2)}) async-start(f32[16,32,4,1,256]{4,3,2,1,0:T(1,128)} %broadcast_in_dim.4), calls=%async_computation | async-start | bytes 4194304 | tf_op jit(solution)/shard_map/all_to_all | solution.py:9
  18.5 198.2 %all-gather.3.cloned.1.call-start = ((), (), s32[]{:S(2)}) async-start(), calls=%async_computation.5 | async-start | bytes 2228224 | tf_op jit(solution)/shard_map/all_gather | solution.py:88
  99.7 4.0 copy-start
  169.4 146.5 %all-gather.5.cloned.1.call-start = ((), (), s32[]{:S(2)}) async-start(), calls=%async_computation.6 | async-start | bytes 2785280 | tf_op jit(solution)/shard_map/all_gather | solution.py:92
  206.8 9.2 %copy-start.4 = (f32[32,6,1,256]{3,2,1,0:T(1,128)S(1)}, f32[32,6,1,256]{3,2,1,0:T(1,128)}, u32[]{:S(2)}) copy-start(f32[32,6,1,256]{3,2,1,0:T(1,128)} %param.9) | copy-start | bytes 589828
  216.7 13.7 %copy-start.2 = (f32[512,512]{1,0:T(8,128)}, f32[512,512]{1,0:T(8,128)S(1)}, u32[]{:S(2)}) copy-start(f32[512,512]{1,0:T(8,128)S(1)} %select_maximum_fusion) | copy-start | bytes 3145732
  279.3 167.4 %reduce-scatter.2.cloned.1.call-start = ((), (), s32[]{:S(2)}) async-start(), calls=%async_computation.7 | async-start | bytes 2506752 | tf_op jit(solution)/shard_map/reduce_scatter | solution.py:38
  356.7 2.2 copy-start.1
  358.8 7.0 %copy-start.3 = (f32[32,1024]{1,0:T(8,128)S(1)}, f32[32,1024]{1,0:T(8,128)}, u32[]{:S(2)}) copy-start(f32[32,1024]{1,0:T(8,128)} %reduce_sum.18) | copy-start | bytes 393220
Sparse Core Ops, SparseCore 0:
  169.5 37.7 all-gather.2
  279.4 36.4 all-gather.4
  369.4 77.3 reduce-scatter.1
where the time goes:
time: 464 us; the launch traced here: 457 us
  blocking collectives  137 us (30%)
  waiting for transfers between devices  113 us (24%)
  other arithmetic  103 us (22%)
  matrix products  41.4 us (9%)
  local copies, waits for them, and re-layouts  40.7 us (9%)
  between operations  14.5 us (3%)
  starting transfers between devices  7.6 us (2%)
    all_to_all x2, blocking collectives, sum_at_owner(): lax.all_to_all(parts, axis, split_axis=0, concat_axis=0, tiled=True)  103 us
    reduce_scatter x1, waiting for transfers between devices, in_one_piece(): result = lax.psum_scatter(both, axis, scatter_dimension=dim, tiled=True)  76.6 us
    unnamed x3, other arithmetic  52.1 us
    all_gather x1, waiting for transfers between devices, per_device(): lax.all_gather(kept_cols, 'prow', axis=2, tiled=True).reshape(x_rows, -1)  36.6 us
    all_to_all x1, blocking collectives, per_device(): lax.all_to_all(head_cols.reshape(x_rows, col_blocks, lax.axis_size('pcol'...  33.8 us
    dot_general x6, matrix products, matmul_hi(): jnp.dot(left, right, precision=lax.Precision.HIGHEST, preferred_element_t...  29.3 us
    unnamed x19, local copies, waits for them, and re-layouts  22.7 us
    another operation x2, other arithmetic, invert_diag(): lax.linalg.triangular_solve(diag_bottom, identity, left_side=True, lower=...  20.7 us
  transfers between devices with their start and end apart: 4, of which 2 were waited for; matrix products, arithmetic and copies ran while one was open for 26% of the time, Pallas kernels for 0%

commit v1 on v0

--- a/solution.py
+++ b/solution.py
@@ -89,7 +89,9 @@
     x_local = sum_at_owner(product + side_term, "pcol", 0)
     x_slab = x_local.reshape(x_rows, h_blocks, 1, block_size)
     kept_cols = x_slab[:, : prev_blocks + 1]
-    widened = lax.all_gather(kept_cols, "prow", axis=2, tiled=True).reshape(x_rows, -1)
+    widened = jnp.concatenate(
+        lax.all_to_all(jnp.stack([kept_cols] * lax.axis_size("prow")), "prow", 0, 0), axis=2
+    ).reshape(x_rows, -1)
     prev_rows = prev_blocks * block_size * lax.axis_size("prow")
     head_cols = widened[:, :prev_rows]
     tail_cols = widened[:, prev_rows : prev_rows + slab_rows]

time: 464 us -> 490 us (1.056)
  blocking collectives: 137 us -> 200 us
  waiting for transfers between devices: 113 us -> 76.1 us
    all_to_all x0 -> x1, blocking collectives: none -> 64.4 us  [per_device(): lax.all_to_all(jnp.stack([kept_cols] * lax.axis_size('prow')), 'prow', 0, 0)]
    all_gather x1 -> x0, waiting for transfers between devices: 36.6 us -> none  [per_device(): lax.all_gather(kept_cols, 'prow', axis=2, tiled=True).reshape(x_rows, -1)]
    unnamed x19 -> x20, local copies, waits for them, and re-layouts: 22.7 us -> 21.2 us
  transfers between devices with their start and end apart: 4 -> 3, of which waited for: 2 -> 1; matrix products, arithmetic and copies ran while one was open for 26% -> 25% of each run, Pallas kernels for 0% -> 0%
where the time goes in v1:
time: 490 us; the launch traced here: 483 us
  blocking collectives  200 us (41%)
  other arithmetic  103 us (21%)
  waiting for transfers between devices  76.1 us (16%)
  matrix products  41.4 us (8%)
  local copies, waits for them, and re-layouts  40.3 us (8%)
  between operations  14.8 us (3%)
  starting transfers between devices  7.56 us (2%)
    all_to_all x2, blocking collectives, sum_at_owner(): lax.all_to_all(parts, axis, split_axis=0, concat_axis=0, tiled=True)  103 us
    reduce_scatter x1, waiting for transfers between devices, in_one_piece(): result = lax.psum_scatter(both, axis, scatter_dimension=dim, tiled=True)  76.1 us
    all_to_all x1, blocking collectives, per_device(): lax.all_to_all(jnp.stack([kept_cols] * lax.axis_size('prow')), 'prow', 0, 0)  64.4 us
    unnamed x3, other arithmetic  52.1 us
    all_to_all x1, blocking collectives, per_device(): lax.all_to_all(head_cols.reshape(x_rows, col_blocks, lax.axis_size('pcol'...  32.6 us
    dot_general x6, matrix products, matmul_hi(): jnp.dot(left, right, precision=lax.Precision.HIGHEST, preferred_element_t...  29.3 us
    unnamed x20, local copies, waits for them, and re-layouts  21.2 us
    another operation x2, other arithmetic, invert_diag(): lax.linalg.triangular_solve(diag_bottom, identity, left_side=True, lower=...  20.7 us
  transfers between devices with their start and end apart: 3, of which 1 were waited for; matrix products, arithmetic and copies ran while one was open for 25% of the time, Pallas kernels for 0%

profile of v1, /device:TPU:2, one launch (start us, length us, event | category | flops | bytes accessed | tf_op | source)
XLA Modules:
  0.0 483.0 jit_solution(12511943435566105362)
XLA Ops:
  8.1 2.9 broadcast_in_dim.4
  11.1 7.5 %all-to-all-start = ((f32[16,32,4,1,256]{4,3,2,1,0:T(1,128)}), f32[16,32,4,1,256]{4,3,2,1,0:T(1,128)S(1)}, u32[]{:S(2)}, u32[]{:S(2)}) async-start(f32[16,32,4,1,256]{4,3,2,1,0:T(1,128)} %broadcast_in_dim.4), calls=%async_computation | async-start | bytes 4194304 | tf_op jit(solution)/shard_map/all_to_all | solution.py:9
  19.8 3.8 while.4
  23.6 19.7 %custom-call.4 = f32[2,128,128]{1,2,0:T(8,128)S(1)} custom-call(f32[2,128,128]{2,1,0:T(8,128)S(1)} %get-tuple-element.18), custom_call_target="InvertDiagBlocksLowerTriangular" | custom-call | tf_op jit(solution)/shard_map/triangular_solve/custom-call.1 | solution.py:61
  43.3 4.0 while.5
  47.3 19.7 %custom-call.5 = f32[2,128,128]{1,2,0:T(8,128)S(1)} custom-call(f32[2,128,128]{2,1,0:T(8,128)S(1)} %get-tuple-element.19), custom_call_target="InvertDiagBlocksLowerTriangular" | custom-call | tf_op jit(solution)/shard_map/triangular_solve/custom-call.1 | solution.py:62
  67.0 14.2 %reduce.1 = f32[4,256,4,256]{3,2,1,0:T(4,128)} reduce(f32[4,1,256,4,1,256]{5,4,3,2,1,0:T(1,128)} %param.7, f32[]{:T(128)} %constant.47), dimensions={1,4}, to_apply=%param.7.reduce_sub_computation | reduce | bytes 8388612 | tf_op args[0]
  81.2 5.2 %copy.43 = f32[128,8,4,256]{3,1,2,0:T(8,128)} copy(f32[128,8,4,256]{3,2,1,0:T(4,128)} %bitcast.87) | data formatting | bytes 8388608
  90.2 7.4 %reduce = f32[16,32,4,256]{3,2,1,0:T(4,128)} reduce(f32[16,32,4,1,256]{4,3,2,1,0:T(1,128)S(1)} %all-to-all-done, f32[]{:T(128)} %constant.47), dimensions={3}, to_apply=%all_to_all.23.reduce_sub_computation | reduce | bytes 4194308 | tf_op jit(solution)/shard_map/all_to_all | solution.py:9
  97.6 2.1 copy.42
  99.7 4.0 fusion.22
  103.7 6.9 %convolution_negate_fusion = f32[512,1024]{1,0:T(8,128)S(1)} fusion(f32[512,1024]{1,0:T(8,128)S(1)} %fusion.22, f32[1024,1024]{1,0:T(8,128)S(1)} %bitcast.82), kind=kOutput, calls=%fused_computation.6 | convolution fusion | flops 6442975232 | bytes 8388608 | tf_op jit(solution)/shard_map/dot_general | solution.py:43
  110.6 58.0 %all_to_all.37 = f32[16,32,1024]{2,1,0:T(8,128)S(1)} all-to-all(f32[16,32,1024]{2,1,0:T(8,128)S(1)} %bitcast.95), channel_id=1, replica_groups=mesh['prow'=16,'pcol'=16] {'prow'}, dimensions={0} | all-to-all | bytes 4194304 | tf_op jit(solution)/shard_map/all_to_all | solution.py:31
  169.5 37.4 %reduce.2 = f32[4,256,6,256]{3,2,1,0:T(8,128)} reduce(f32[4,1,256,6,1,256]{5,4,3,2,1,0:T(1,128)} %param.8, f32[]{:T(128)} %constant.47), dimensions={1,4}, to_apply=%param.8.reduce_sub_computation | reduce | bytes 12582916 | tf_op args[1]
  206.8 9.2 %copy.44 = f32[128,8,6,256]{3,1,2,0:T(8,128)} copy(f32[128,8,6,256]{3,2,1,0:T(8,128)} %bitcast.84) | data formatting | bytes 12582912
  216.8 13.7 %fusion.25 = f32[512,1536]{1,0:T(8,128)S(1)} fusion(f32[512,1024]{1,0:T(8,128)} %all-gather.2.cloned.1.call-done, f32[1024,1536]{1,0:T(8,128)} %bitcast.96), kind=kOutput, calls=%fused_computation.48 | convolution fusion | flops 9663676416 | bytes 11534336 | tf_op jit(solution)/shard_map/dot_general | solution.py:43
  230.4 2.8 convolution_add_fusion
  233.2 45.1 %all_to_all.38 = f32[16,32,1536]{2,1,0:T(8,128)S(1)} all-to-all(f32[16,32,1536]{2,1,0:T(8,128)S(1)} %bitcast.88), channel_id=1, replica_groups=mesh['prow'=16,'pcol'=16] {'pcol'}, dimensions={0} | all-to-all | bytes 6291456 | tf_op jit(solution)/shard_map/all_to_all | solution.py:31
  278.9 64.4 %all_to_all.35 = f32[16,32,5,1,256]{4,1,3,2,0:T(8,128)S(1)} all-to-all(f32[16,32,5,1,256]{4,1,3,2,0:T(8,128)S(1)} %stack.2), channel_id=1, replica_groups=mesh['prow'=16,'pcol'=16] {'prow'}, dimensions={0} | all-to-all | bytes 5242880 | tf_op jit(solution)/shard_map/all_to_all | solution.py:93
  344.9 1.8 reshape_reshape.7
  350.3 32.6 %all_to_all.36 = f32[32,4,16,256]{3,1,0,2:T(4,128)S(1)} all-to-all(f32[32,4,16,256]{3,1,0,2:T(4,128)S(1)} %copy.35), channel_id=1, replica_groups=mesh['prow'=16,'pcol'=16] {'pcol'}, dimensions={2} | all-to-all | bytes 4194304 | tf_op jit(solution)/shard_map/all_to_all | solution.py:98
  385.1 7.0 %fusion.26 = f32[512,1024]{1,0:T(8,128)S(1)} fusion(f32[512,1024]{1,0:T(8,128)S(1)} %bitcast.85, f32[1024,1024]{1,0:T(8,128)S(1)} %bitcast.83), kind=kOutput, calls=%fused_computation.49 | convolution fusion | flops 6442450944 | bytes 8388608 | tf_op jit(solution)/shard_map/dot_general | solution.py:47
  392.0 1.8 fusion.27
  396.3 76.1 %reduce-scatter.2.cloned.1.call-done = f32[32,1056]{1,0:T(8,128)} async-done(((f32[512,1056]{1,0:T(8,128)}), f32[32,1056]{1,0:T(8,128)}) %reduce-scatter.2.cloned.1.call-update) | async-done | bytes 135184 | tf_op jit(solution)/shard_map/reduce_scatter | solution.py:38
  (65 shorter events, 28.9 us)
Async XLA Ops:
  11.1 79.2 %all-to-all-start = ((f32[16,32,4,1,256]{4,3,2,1,0:T(1,128)}), f32[16,32,4,1,256]{4,3,2,1,0:T(1,128)S(1)}, u32[]{:S(2)}, u32[]{:S(2)}) async-start(f32[16,32,4,1,256]{4,3,2,1,0:T(1,128)} %broadcast_in_dim.4), calls=%async_computation | async-start | bytes 4194304 | tf_op jit(solution)/shard_map/all_to_all | solution.py:9
  18.5 198.2 %all-gather.2.cloned.1.call-start = ((), (), s32[]{:S(2)}) async-start(), calls=%async_computation.6 | async-start | bytes 2228224 | tf_op jit(solution)/shard_map/all_gather | solution.py:88
  99.7 4.0 copy-start
  169.4 303.0 %reduce-scatter.2.cloned.1.call-start = ((), (), s32[]{:S(2)}) async-start(), calls=%async_computation.7 | async-start | bytes 2506752 | tf_op jit(solution)/shard_map/reduce_scatter | solution.py:38
  206.8 9.2 %copy-start.5 = (f32[32,6,1,256]{3,2,1,0:T(1,128)S(1)}, f32[32,6,1,256]{3,2,1,0:T(1,128)}, u32[]{:S(2)}) copy-start(f32[32,6,1,256]{3,2,1,0:T(1,128)} %param.9) | copy-start | bytes 589828
  216.7 13.7 %copy-start.3 = (f32[512,512]{1,0:T(8,128)}, f32[512,512]{1,0:T(8,128)S(1)}, u32[]{:S(2)}) copy-start(f32[512,512]{1,0:T(8,128)S(1)} %select_maximum_fusion) | copy-start | bytes 3145732
  346.7 1.6 slice-start
  382.9 2.2 copy-start.1
  385.1 7.0 %copy-start.4 = (f32[32,1024]{1,0:T(8,128)S(1)}, f32[32,1024]{1,0:T(8,128)}, u32[]{:S(2)}) copy-start(f32[32,1024]{1,0:T(8,128)} %reduce_sum.18) | copy-start | bytes 393220
  395.4 78.7 %copy-start.2 = (f32[32,20480]{1,0:T(8,128)S(1)}, f32[32,20480]{1,0:T(8,128)}, u32[]{:S(2)}) copy-start(f32[32,20480]{1,0:T(8,128)} %reshape_reshape.7) | copy-start | bytes 7864324
Sparse Core Ops, SparseCore 0:
  169.5 37.7 all-gather.1
  395.6 76.7 reduce-scatter.1
